TPU v7x, 32 devices: a whole 2x2x4 slice. The times are simulated.
32 devices in a mesh: section: 2 (over y), dp: 16 (over z, x, core).
Axes of the slice: x: 2, y: 2, z: 4, core: 2. Of those that a mesh axis runs over, the one named last changes fastest.
Arguments:
- activations: bfloat16 [2, 4, 16, 14336], P('section', None, 'dp'), may hold values from -6 to 6
- out_grads: bfloat16 [2, 4, 16, 4096], P('section', None, 'dp'), may hold values from -6 to 6
- basis_in: bfloat16 [2, 14336, 1024], P('section', 'dp'), may hold values from -0.046875 to 0.046875
- basis_out: bfloat16 [2, 4096, 1024], P('section', 'dp'), may hold values from -0.09375 to 0.09375
- eigen_values: float32 [2, 1024, 1024], P('section', 'dp'), may hold values from 0.02 to 2
- query_proj: bfloat16 [2, 8, 1024, 1024], P('section', None, 'dp'), may hold values from -0.046875 to 0.046875
- lengths: int32 [4], replicated, may hold values from 4 to 16
- seq_rows: int32 [4], replicated, may hold values from 0 to 127
- prior_table: float32 [128, 8], P('dp'), may hold values from -6 to 6
Outputs:
- influence: float32 [2, 128, 8], P('section', 'dp')
All inputs are finite; a program needn't handle non-finite values.
Results may differ from a plain program's by a relative error of at most 0.01.
Values may be sent and summed in bfloat16 or wider, within the bound.
No kernel may reach another device: no remote copies, remote signals or barrier semaphores. Data moves between devices by JAX's collectives and lax.ppermute only.
A program may use at most 64 MiB of HBM per device.

v0:
```python
import jax
import jax.numpy as jnp
from jax import lax
from jax.sharding import PartitionSpec as P

DAMPING = 0.01


def entering(value, axis, join, neutral):
    count, mine = (lax.axis_size(axis), lax.axis_index(axis))
    pieces = lax.all_gather(value, axis)
    running = jnp.full_like(value, 0) + jnp.asarray(neutral, value.dtype)

    def step(position, running):
        longer = join(running, pieces[position])
        return jnp.where(position < mine, longer, running)

    return lax.fori_loop(0, count - 1, step, running)


def add_pair(earlier, latter):
    return earlier + latter


def per_device(
    activations,
    out_grads,
    basis_in,
    basis_out,
    eigen_values,
    query_proj,
    lengths,
    seq_rows,
    prior_table,
):
    micro = activations.shape[1]
    cols_acts, cols_grads = (
        lax.all_to_all(activations[0], "dp", split_axis=2, concat_axis=1, tiled=True),
        lax.all_to_all(out_grads[0], "dp", split_axis=2, concat_axis=1, tiled=True),
    )
    slots = cols_acts.shape[1]
    rank_size = basis_in.shape[2]
    act_part = jnp.dot(
        cols_acts.reshape(micro * slots, cols_acts.shape[2]),
        basis_in[0],
        preferred_element_type=jnp.float32,
    )
    grad_part = jnp.dot(
        cols_grads.reshape(micro * slots, cols_grads.shape[2]),
        basis_out[0],
        preferred_element_type=jnp.float32,
    )
    grad_share = lax.psum_scatter(grad_part, "dp", scatter_dimension=1, tiled=True).astype(
        jnp.bfloat16
    )
    act_proj = lax.psum(act_part, "dp").astype(jnp.bfloat16)
    block_rows = grad_share.shape[1]
    position = jnp.arange(slots, dtype=jnp.int32)
    live_mask = (position[None, :] < lengths[:, None]).reshape(micro * slots, 1)
    grad_share = jnp.where(live_mask, grad_share, jnp.zeros_like(grad_share))
    inverse_len = 1.0 / lengths.astype(jnp.float32)
    seq_block = (
        jnp.einsum(
            "mti,mtj->mij",
            grad_share.reshape(micro, slots, block_rows),
            act_proj.reshape(micro, slots, rank_size),
            preferred_element_type=jnp.float32,
        )
        * inverse_len[:, None, None]
    )
    precond = (query_proj[0].astype(jnp.float32) / (eigen_values[0][None] + DAMPING)).astype(
        jnp.bfloat16
    )
    partial_value = jnp.einsum(
        "mij,qij->mq", seq_block, precond.astype(jnp.float32), precision=lax.Precision.HIGHEST
    )
    table_rows = prior_table.shape[0]
    first_row = lax.axis_index("dp") * table_rows
    summed = lax.psum(partial_value, "dp")
    before = entering(summed, "section", add_pair, jnp.zeros_like(summed))
    owner_mask = (
        seq_rows[None, :] == (first_row + jnp.arange(table_rows, dtype=jnp.int32))[:, None]
    ).astype(jnp.float32)
    result = prior_table + jnp.dot(owner_mask, before + summed, precision=lax.Precision.HIGHEST)
    return result[None]


def solution(mesh):
    return jax.shard_map(
        per_device,
        mesh=mesh,
        in_specs=(
            P("section", None, "dp", None),
            P("section", None, "dp", None),
            P("section", "dp", None),
            P("section", "dp", None),
            P("section", "dp", None),
            P("section", None, "dp", None),
            P(),
            P(),
            P("dp", None),
        ),
        out_specs=P("section", "dp", None),
        check_vma=False,
    )
```

profile of v0, /device:TPU:0, one launch (start us, length us, event | category | flops | bytes accessed | tf_op | source)
XLA Modules:
  0.0 303.3 jit_solution(3628222360008374152)
XLA Ops:
  6.5 5.0 %copy.14 = bf16[4,1,4096]{0,1,2:T(2,128)(2,1)} copy(bf16[4,1,4096]{2,0,1:T(4,128)(2,1)} %bitcast.47) | data formatting | bytes 65536 | tf_op jit(solution)/shard_map/squeeze | solution.py:39
  12.1 23.5 %reduce = bf16[4096,4]{1,0:T(8,128)(2,1)S(1)} reduce(bf16[4096,1,4]{2,1,0:T(2,128)(2,1)} %bitcast.42, bf16[]{:T(256)} %broadcast.36), dimensions={1}, to_apply=%bitcast.32.reduce_sub_computation | reduce | bytes 65538
  35.5 2.6 reshape.67
  38.1 7.4 %all-to-all-start = ((bf16[16,2,512]{2,1,0:T(2,128)(2,1)}), bf16[16,2,512]{2,1,0:T(2,128)(2,1)S(1)}, u32[]{:S(2)}, u32[]{:S(2)}) async-start(bf16[16,2,512]{2,1,0:T(2,128)(2,1)} %reshape.67), calls=%async_computation | async-start | bytes 65536 | tf_op jit(solution)/shard_map/all_to_all | solution.py:39
  45.6 0.5 convert_divide_fusion.1
  46.2 11.6 %copy.16 = bf16[4,1,14336]{0,1,2:T(2,128)(2,1)} copy(bf16[4,1,14336]{2,0,1:T(4,128)(2,1)S(1)} %bitcast.45) | data formatting | bytes 229376 | tf_op jit(solution)/shard_map/squeeze | solution.py:38
  57.7 79.8 %reduce.1 = bf16[14336,4]{1,0:T(8,128)(2,1)} reduce(bf16[14336,1,4]{2,1,0:T(2,128)(2,1)} %bitcast.41, bf16[]{:T(256)} %broadcast.36), dimensions={1}, to_apply=%bitcast.34.reduce_sub_computation | reduce | bytes 229378
  137.6 8.3 %reshape.69 = bf16[16,2,1792]{2,1,0:T(2,128)(2,1)} reshape(bf16[14336,4]{1,0:T(8,128)(2,1)} %reduce.1) | data formatting | bytes 229376
  145.8 0.6 lt.31
  146.5 1.5 fusion
  148.0 0.5 iota_add_fusion
  148.6 6.0 %all-to-all-start.1 = ((bf16[16,2,1792]{2,1,0:T(2,128)(2,1)}), bf16[16,2,1792]{2,1,0:T(2,128)(2,1)S(1)}, u32[]{:S(2)}, u32[]{:S(2)}) async-start(bf16[16,2,1792]{2,1,0:T(2,128)(2,1)} %reshape.69), calls=%async_computation.1 | async-start | bytes 229376 | tf_op jit(solution)/shard_map/all_to_all | solution.py:38
  154.6 4.5 %reshape.68 = bf16[4096,1,4]{2,1,0:T(2,128)(2,1)} reshape(bf16[16,2,512]{2,1,0:T(2,128)(2,1)S(1)} %all-to-all-done) | data formatting | bytes 65536
  159.2 4.5 %copy.15 = bf16[4,1,4096]{2,0,1:T(4,128)(2,1)S(1)} copy(bf16[4,1,4096]{0,1,2:T(2,128)(2,1)} %bitcast.43) | data formatting | bytes 65536 | tf_op jit(solution)/shard_map/all_to_all | solution.py:39
  163.7 0.6 reshape.47
  164.4 1.9 convolution_bitcast_fusion
  166.3 11.5 %reshape.70 = bf16[14336,1,4]{2,1,0:T(2,128)(2,1)} reshape(bf16[16,2,1792]{2,1,0:T(2,128)(2,1)S(1)} %all-to-all-done.1) | data formatting | bytes 229376
  177.8 13.9 %copy.17 = bf16[4,1,14336]{2,0,1:T(4,128)(2,1)S(1)} copy(bf16[4,1,14336]{0,1,2:T(2,128)(2,1)} %bitcast.40) | data formatting | bytes 229376 | tf_op jit(solution)/shard_map/all_to_all | solution.py:38
  192.3 64.6 %all-reduce.1 = bf16[64,1024]{1,0:T(8,128)(2,1)S(1)} all-reduce(f32[64,1024]{1,0:T(8,128)S(1)} %fusion.1), channel_id=1, replica_groups=mesh['section'=2,'dp'=16] {'dp'}, use_global_device_ids=true, to_apply=%region_1.0 | all-reduce | flops 65536 | bytes 393216 | tf_op jit(solution)/shard_map/psum | solution.py:56
  257.0 0.8 copy.21
  258.3 3.5 %convolution_bitcast_fusion.1 = f32[4,8]{1,0:T(4,128)S(1)} fusion(bf16[8,64,1024]{2,1,0:T(8,128)(2,1)S(1)} %fusion, f32[4,64,1024]{2,1,0:T(8,128)S(1)} %convolution_multiply_fusion), kind=kOutput, calls=%fused_computation.8 | convolution fusion | flops 25165824 | bytes 2097280 | tf_op jit(solution)/shard_map/mij,qij->mq/dot_general | solution.py:74
  261.8 29.5 %psum.15 = f32[4,8]{1,0:T(4,128)S(1)} all-reduce(f32[4,8]{1,0:T(4,128)S(1)} %convolution_bitcast_fusion.1), channel_id=1, replica_groups=mesh['section'=2,'dp'=16] {'dp'}, use_global_device_ids=true, to_apply=%region_2.3 | all-reduce | flops 32 | bytes 256 | tf_op jit(solution)/shard_map/psum | solution.py:79
  291.3 4.4 %all-gather.1 = f32[2,4,8]{2,1,0:T(4,128)S(1)} all-gather(f32[1,4,8]{2,1,0:T(4,128)S(1)} %bitcast.49), channel_id=2, replica_groups=mesh['section'=2,'dp'=16] {'section'}, dimensions={0}, use_global_device_ids=true | all-gather | bytes 384 | tf_op jit(solution)/shard_map/all_gather | solution.py:11
  295.6 0.8 fusion.3
  (32 shorter events, 1.7 us)
Async XLA Ops:
  6.5 185.3 %copy-start = (bf16[1,896,1024]{2,1,0:T(8,128)(2,1)S(1)}, bf16[1,896,1024]{2,1,0:T(8,128)(2,1)}, u32[]{:S(2)}) copy-start(bf16[1,896,1024]{2,1,0:T(8,128)(2,1)} %param.11) | copy-start | bytes 5505028
  12.1 33.5 %copy-start.7 = (s32[4]{0:T(128)S(1)}, s32[4]{0:T(128)}, u32[]{:S(2)}) copy-start(s32[4]{0:T(128)} %param.15) | copy-start | bytes 52
  12.1 34.1 %copy-start.3 = (bf16[1,4,1,14336]{3,1,2,0:T(4,128)(2,1)S(1)}, bf16[1,4,1,14336]{3,1,2,0:T(4,128)(2,1)}, u32[]{:S(2)}) copy-start(bf16[1,4,1,14336]{3,1,2,0:T(4,128)(2,1)} %param.9) | copy-start | bytes 344068
  38.1 110.4 %all-to-all-start = ((bf16[16,2,512]{2,1,0:T(2,128)(2,1)}), bf16[16,2,512]{2,1,0:T(2,128)(2,1)S(1)}, u32[]{:S(2)}, u32[]{:S(2)}) async-start(bf16[16,2,512]{2,1,0:T(2,128)(2,1)} %reshape.67), calls=%async_computation | async-start | bytes 65536 | tf_op jit(solution)/shard_map/all_to_all | solution.py:39
  137.6 8.9 %copy-start.2 = (f32[1,64,1024]{2,1,0:T(8,128)S(1)}, f32[1,64,1024]{2,1,0:T(8,128)}, u32[]{:S(2)}) copy-start(f32[1,64,1024]{2,1,0:T(8,128)} %param.13) | copy-start | bytes 786436
  148.6 17.7 %all-to-all-start.1 = ((bf16[16,2,1792]{2,1,0:T(2,128)(2,1)}), bf16[16,2,1792]{2,1,0:T(2,128)(2,1)S(1)}, u32[]{:S(2)}, u32[]{:S(2)}) async-start(bf16[16,2,1792]{2,1,0:T(2,128)(2,1)} %reshape.69), calls=%async_computation.1 | async-start | bytes 229376 | tf_op jit(solution)/shard_map/all_to_all | solution.py:38
  154.6 9.8 %copy-start.1 = (bf16[1,256,1024]{2,1,0:T(8,128)(2,1)S(1)}, bf16[1,256,1024]{2,1,0:T(8,128)(2,1)}, u32[]{:S(2)}) copy-start(bf16[1,256,1024]{2,1,0:T(8,128)(2,1)} %param.12) | copy-start | bytes 1572868
  154.6 102.4 %reduce-scatter.4.cloned.1.call-start = ((), (), s32[]{:S(2)}) async-start(), calls=%async_computation.3 | async-start | bytes 557056
  191.7 66.1 %copy-start.5 = (pred[64]{0:T(512)(128)(4,1)S(1)}, pred[64]{0:T(512)(128)(4,1)}, u32[]{:S(2)}) copy-start(pred[64]{0:T(512)(128)(4,1)} %lt.31) | copy-start | bytes 196
  191.7 66.1 %copy-start.4 = (f32[4]{0:T(128)S(1)}, f32[4]{0:T(128)}, u32[]{:S(2)}) copy-start(f32[4]{0:T(128)} %convert_divide_fusion.1) | copy-start | bytes 52
  192.3 103.3 %copy-start.6 = (f32[8,8]{1,0:T(8,128)S(1)}, f32[8,8]{1,0:T(8,128)}, u32[]{:S(2)}) copy-start(f32[8,8]{1,0:T(8,128)} %param.17) | copy-start | bytes 772
  192.3 103.3 %copy-start.8 = (s32[4]{0:T(128)S(1)}, s32[4]{0:T(128)}, u32[]{:S(2)}) copy-start(s32[4]{0:T(128)} %param.16) | copy-start | bytes 52
  192.3 103.3 %copy-start.9 = (s32[8]{0:T(128)S(1)}, s32[8]{0:T(128)}, u32[]{:S(2)}) copy-start(s32[8]{0:T(128)} %iota_add_fusion) | copy-start | bytes 100
Sparse Core Ops, SparseCore 0:
  166.4 57.5 reduce-scatter.3
where the time goes:
time: 304 us; the launch traced here: 303 us
  other arithmetic  106 us (35%)
  blocking collectives  98.4 us (32%)
  local copies, waits for them, and re-layouts  64.7 us (21%)
  between operations  13.6 us (4%)
  starting transfers between devices  13.4 us (4%)
  matrix products  6.96 us (2%)
    unnamed x2, other arithmetic  103 us
    psum x1, blocking collectives, per_device(): act_proj = lax.psum(act_part, 'dp').astype(jnp.bfloat16)  64.6 us
    psum x1, blocking collectives, per_device(): summed = lax.psum(partial_value, 'dp')  29.5 us
    unnamed x26, local copies, waits for them, and re-layouts  28.3 us
    all_to_all x1, local copies, waits for them, and re-layouts, per_device(): lax.all_to_all(activations[0], 'dp', split_axis=2, concat_axis=1, tiled=T...  13.9 us
    squeeze x1, local copies, waits for them, and re-layouts, per_device(): activations[0]  11.6 us
    all_to_all x1, starting transfers between devices, per_device(): lax.all_to_all(out_grads[0], 'dp', split_axis=2, concat_axis=1, tiled=True)  7.39 us
  transfers between devices with their start and end apart: 3, of which 0 were waited for; matrix products, arithmetic and copies ran while one was open for 46% of the time, Pallas kernels for 0%

commit v1 on v0

--- a/solution.py
+++ b/solution.py
@@ -53,7 +53,7 @@
     grad_share = lax.psum_scatter(grad_part, "dp", scatter_dimension=1, tiled=True).astype(
         jnp.bfloat16
     )
-    act_proj = lax.psum(act_part, "dp").astype(jnp.bfloat16)
+    act_proj = jnp.sum(lax.all_gather(act_part, "dp"), axis=0).astype(jnp.bfloat16)
     block_rows = grad_share.shape[1]
     position = jnp.arange(slots, dtype=jnp.int32)
     live_mask = (position[None, :] < lengths[:, None]).reshape(micro * slots, 1)

time: 304 us -> 322 us (1.059)
  waiting for transfers between devices: 0.04 us -> 79.6 us
  blocking collectives: 98.4 us -> 35.5 us
    psum x1 -> x0, blocking collectives: 64.6 us -> none  [per_device(): act_proj = lax.psum(act_part, 'dp').astype(jnp.bfloat16)]
    all_gather x0 -> x1, waiting for transfers between devices: none -> 50.7 us  [per_device(): lax.all_gather(act_part, 'dp')]
    unnamed x2 -> x3, waiting for transfers between devices: 0.04 us -> 29 us
    unnamed x26 -> x20, local copies, waits for them, and re-layouts: 28.3 us -> 28.3 us
  transfers between devices with their start and end apart: 3 -> 4, of which waited for: 0 -> 2; matrix products, arithmetic and copies ran while one was open for 46% -> 43% of each run, Pallas kernels for 0% -> 0%
where the time goes in v1:
time: 322 us; the launch traced here: 321 us
  other arithmetic  108 us (34%)
  waiting for transfers between devices  79.6 us (25%)
  local copies, waits for them, and re-layouts  63.6 us (20%)
  blocking collectives  35.5 us (11%)
  starting transfers between devices  13.7 us (4%)
  between operations  13.6 us (4%)
  matrix products  6.9 us (2%)
    unnamed x2, other arithmetic  103 us
    all_gather x1, waiting for transfers between devices, per_device(): lax.all_gather(act_part, 'dp')  50.7 us
    psum x1, blocking collectives, per_device(): summed = lax.psum(partial_value, 'dp')  31.2 us
    unnamed x3, waiting for transfers between devices  29 us
    unnamed x20, local copies, waits for them, and re-layouts  28.3 us
    all_to_all x1, local copies, waits for them, and re-layouts, per_device(): lax.all_to_all(activations[0], 'dp', split_axis=2, concat_axis=1, tiled=T...  13.9 us
    squeeze x1, local copies, waits for them, and re-layouts, per_device(): activations[0]  11.6 us
    all_to_all x1, starting transfers between devices, per_device(): lax.all_to_all(out_grads[0], 'dp', split_axis=2, concat_axis=1, tiled=True)  7.39 us
  transfers between devices with their start and end apart: 4, of which 2 were waited for; matrix products, arithmetic and copies ran while one was open for 43% of the time, Pallas kernels for 0%

profile of v1, /device:TPU:0, one launch (start us, length us, event | category | flops | bytes accessed | tf_op | source)
XLA Modules:
  0.0 320.5 jit_solution(16474796855578619910)
XLA Ops:
  6.5 5.0 %copy.14 = bf16[4,1,4096]{0,1,2:T(2,128)(2,1)} copy(bf16[4,1,4096]{2,0,1:T(4,128)(2,1)} %bitcast.49) | data formatting | bytes 65536 | tf_op jit(solution)/shard_map/squeeze | solution.py:39
  11.5 0.5 broadcast.36
  12.1 23.5 %reduce = bf16[4096,4]{1,0:T(8,128)(2,1)S(1)} reduce(bf16[4096,1,4]{2,1,0:T(2,128)(2,1)} %bitcast.43, bf16[]{:T(256)} %broadcast.36), dimensions={1}, to_apply=%bitcast.33.reduce_sub_computation | reduce | bytes 65538
  35.5 2.6 reshape.67
  38.1 7.4 %all-to-all-start = ((bf16[16,2,512]{2,1,0:T(2,128)(2,1)}), bf16[16,2,512]{2,1,0:T(2,128)(2,1)S(1)}, u32[]{:S(2)}, u32[]{:S(2)}) async-start(bf16[16,2,512]{2,1,0:T(2,128)(2,1)} %reshape.67), calls=%async_computation | async-start | bytes 65536 | tf_op jit(solution)/shard_map/all_to_all | solution.py:39
  45.6 11.6 %copy.16 = bf16[4,1,14336]{0,1,2:T(2,128)(2,1)} copy(bf16[4,1,14336]{2,0,1:T(4,128)(2,1)S(1)} %bitcast.47) | data formatting | bytes 229376 | tf_op jit(solution)/shard_map/squeeze | solution.py:38
  57.2 79.8 %reduce.1 = bf16[14336,4]{1,0:T(8,128)(2,1)} reduce(bf16[14336,1,4]{2,1,0:T(2,128)(2,1)} %bitcast.42, bf16[]{:T(256)} %broadcast.36), dimensions={1}, to_apply=%bitcast.35.reduce_sub_computation | reduce | bytes 229378
  137.0 8.2 %reshape.69 = bf16[16,2,1792]{2,1,0:T(2,128)(2,1)} reshape(bf16[14336,4]{1,0:T(8,128)(2,1)} %reduce.1) | data formatting | bytes 229376
  145.3 6.0 %all-to-all-start.1 = ((bf16[16,2,1792]{2,1,0:T(2,128)(2,1)}), bf16[16,2,1792]{2,1,0:T(2,128)(2,1)S(1)}, u32[]{:S(2)}, u32[]{:S(2)}) async-start(bf16[16,2,1792]{2,1,0:T(2,128)(2,1)} %reshape.69), calls=%async_computation.1 | async-start | bytes 229376 | tf_op jit(solution)/shard_map/all_to_all | solution.py:38
  151.3 4.5 %reshape.68 = bf16[4096,1,4]{2,1,0:T(2,128)(2,1)} reshape(bf16[16,2,512]{2,1,0:T(2,128)(2,1)S(1)} %all-to-all-done) | data formatting | bytes 65536
  155.9 4.5 %copy.15 = bf16[4,1,4096]{2,0,1:T(4,128)(2,1)S(1)} copy(bf16[4,1,4096]{0,1,2:T(2,128)(2,1)} %bitcast.44) | data formatting | bytes 65536 | tf_op jit(solution)/shard_map/all_to_all | solution.py:39
  160.4 1.1 convolution_bitcast_fusion
  161.9 11.5 %reshape.70 = bf16[14336,1,4]{2,1,0:T(2,128)(2,1)} reshape(bf16[16,2,1792]{2,1,0:T(2,128)(2,1)S(1)} %all-to-all-done.1) | data formatting | bytes 229376
  173.4 13.9 %copy.17 = bf16[4,1,14336]{2,0,1:T(4,128)(2,1)S(1)} copy(bf16[4,1,14336]{0,1,2:T(2,128)(2,1)} %bitcast.41) | data formatting | bytes 229376 | tf_op jit(solution)/shard_map/all_to_all | solution.py:38
  187.5 1.1 fusion.1
  188.8 1.6 fusion
  190.4 28.9 %reduce-scatter.4.cloned.1.call-done = f32[64,64]{1,0:T(8,128)} async-done(((f32[1024,64]{1,0:T(8,128)}), f32[64,64]{1,0:T(8,128)}) %reduce-scatter.4.cloned.1.call-update) | async-done | bytes 16400
  219.3 0.8 copy.21
  220.3 50.7 %all-gather.5.cloned.1.call-done = f32[1024,1024]{1,0:T(8,128)} async-done(((f32[64,1024]{1,0:T(8,128)}), f32[1024,1024]{1,0:T(8,128)}) %all-gather.5.cloned.1.call-update) | async-done | bytes 4194320 | tf_op jit(solution)/shard_map/all_gather | solution.py:56
  270.9 2.5 reduce_sum.9
  273.8 3.5 %convolution_bitcast_fusion.1 = f32[4,8]{1,0:T(4,128)S(1)} fusion(bf16[8,64,1024]{2,1,0:T(8,128)(2,1)S(1)} %fusion, f32[4,64,1024]{2,1,0:T(8,128)S(1)} %convolution_multiply_fusion), kind=kOutput, calls=%fused_computation.8 | convolution fusion | flops 25165824 | bytes 2097280 | tf_op jit(solution)/shard_map/mij,qij->mq/dot_general | solution.py:74
  277.3 31.2 %psum.7 = f32[4,8]{1,0:T(4,128)S(1)} all-reduce(f32[4,8]{1,0:T(4,128)S(1)} %convolution_bitcast_fusion.1), channel_id=1, replica_groups=mesh['section'=2,'dp'=16] {'dp'}, use_global_device_ids=true, to_apply=%region_2.3 | all-reduce | flops 32 | bytes 256 | tf_op jit(solution)/shard_map/psum | solution.py:79
  308.5 4.4 %all-gather.2 = f32[2,4,8]{2,1,0:T(4,128)S(1)} all-gather(f32[1,4,8]{2,1,0:T(4,128)S(1)} %bitcast.51), channel_id=3, replica_groups=mesh['section'=2,'dp'=16] {'section'}, dimensions={0}, use_global_device_ids=true | all-gather | bytes 384 | tf_op jit(solution)/shard_map/all_gather | solution.py:11
  312.9 0.8 fusion.3
  (29 shorter events, 1.1 us)
Async XLA Ops:
  6.5 180.9 %copy-start = (bf16[1,896,1024]{2,1,0:T(8,128)(2,1)S(1)}, bf16[1,896,1024]{2,1,0:T(8,128)(2,1)}, u32[]{:S(2)}) copy-start(bf16[1,896,1024]{2,1,0:T(8,128)(2,1)} %param.11) | copy-start | bytes 5505028
  12.1 33.5 %copy-start.3 = (bf16[1,4,1,14336]{3,1,2,0:T(4,128)(2,1)S(1)}, bf16[1,4,1,14336]{3,1,2,0:T(4,128)(2,1)}, u32[]{:S(2)}) copy-start(bf16[1,4,1,14336]{3,1,2,0:T(4,128)(2,1)} %param.9) | copy-start | bytes 344068
  38.1 107.1 %all-to-all-start = ((bf16[16,2,512]{2,1,0:T(2,128)(2,1)}), bf16[16,2,512]{2,1,0:T(2,128)(2,1)S(1)}, u32[]{:S(2)}, u32[]{:S(2)}) async-start(bf16[16,2,512]{2,1,0:T(2,128)(2,1)} %reshape.67), calls=%async_computation | async-start | bytes 65536 | tf_op jit(solution)/shard_map/all_to_all | solution.py:39
  145.3 16.6 %all-to-all-start.1 = ((bf16[16,2,1792]{2,1,0:T(2,128)(2,1)}), bf16[16,2,1792]{2,1,0:T(2,128)(2,1)S(1)}, u32[]{:S(2)}, u32[]{:S(2)}) async-start(bf16[16,2,1792]{2,1,0:T(2,128)(2,1)} %reshape.69), calls=%async_computation.1 | async-start | bytes 229376 | tf_op jit(solution)/shard_map/all_to_all | solution.py:38
  151.3 9.2 %copy-start.1 = (bf16[1,256,1024]{2,1,0:T(8,128)(2,1)S(1)}, bf16[1,256,1024]{2,1,0:T(8,128)(2,1)}, u32[]{:S(2)}) copy-start(bf16[1,256,1024]{2,1,0:T(8,128)(2,1)} %param.12) | copy-start | bytes 1572868
  151.3 68.1 %reduce-scatter.4.cloned.1.call-start = ((), (), s32[]{:S(2)}) async-start(), calls=%async_computation.4 | async-start | bytes 557056
  161.6 109.3 %all-gather.5.cloned.1.call-start = ((), (), s32[]{:S(2)}) async-start(), calls=%async_computation.3 | async-start | bytes 4456448 | tf_op jit(solution)/shard_map/all_gather | solution.py:56
  187.3 1.3 copy-start.5
  187.3 1.5 copy-start.2
  273.5 39.4 %copy-start.4 = (f32[8,8]{1,0:T(8,128)S(1)}, f32[8,8]{1,0:T(8,128)}, u32[]{:S(2)}) copy-start(f32[8,8]{1,0:T(8,128)} %param.17) | copy-start | bytes 772
  273.5 39.4 %copy-start.6 = (s32[4]{0:T(128)S(1)}, s32[4]{0:T(128)}, u32[]{:S(2)}) copy-start(s32[4]{0:T(128)} %param.16) | copy-start | bytes 52
Sparse Core Ops, SparseCore 0:
  161.7 57.5 reduce-scatter.3
  221.5 49.3 all-gather.4
